TPU v7x, 32 devices: a whole 2x2x4 slice. The times are simulated.
32 devices in a mesh: section: 1, grp: 16 (over z, x, core), tp: 2 (over y).
Axes of the slice: x: 2, y: 2, z: 4, core: 2. Of those that a mesh axis runs over, the one named last changes fastest.
Arguments:
- partials: bfloat16 [2, 1, 2048, 8192], P('tp', 'section', 'grp'), may hold values from -3 to 3
- residual: bfloat16 [1, 2048, 8192], P('section', 'grp', 'tp'), may hold values from -300 to 300
- norm_gain: bfloat16 [8192], replicated, may hold values from 0.099609375 to 1.8984375
- w_query: bfloat16 [8192, 8192], P('grp', ('section', 'tp')), may hold values from -0.0625 to 0.0625
- w_keyval: bfloat16 [8192, 2048], P('grp', ('section', 'tp')), may hold values from -0.0625 to 0.0625
- bias_query: bfloat16 [8192], P(('section', 'tp')), may hold values from -3 to 3
- bias_keyval: bfloat16 [2048], P(('section', 'tp')), may hold values from -3 to 3
Outputs:
- hidden: bfloat16 [1, 2048, 8192], P('section', 'grp', 'tp')
- query: bfloat16 [1, 2048, 8192], P(None, 'grp', ('section', 'tp'))
- keyval: bfloat16 [1, 2048, 2048], P(None, 'grp', ('section', 'tp'))
All inputs are finite; a program needn't handle non-finite values.
Results may differ from a plain program's by a relative error of at most 0.01.
Values may be sent and summed in bfloat16 or wider, within the bound.
A program may use at most 192 MiB of HBM per device.

v0:
```python
import jax
import jax.numpy as jnp
from jax import lax
from jax.sharding import PartitionSpec as P

epsilon = 1e-06


def local(partials, residual, norm_gain, w_query, w_keyval, bias_query, bias_keyval):
    model_width = norm_gain.shape[0]
    summed = lax.psum_scatter(partials[0], "tp", scatter_dimension=2, tiled=True).astype(
        jnp.float32
    )
    hidden = (residual.astype(jnp.float32) + summed).astype(jnp.bfloat16)
    widened = hidden.astype(jnp.float32)
    squares = lax.psum(jnp.sum(widened * widened, axis=-1), "tp")
    feature_share = widened.shape[2]
    offset = lax.axis_index("tp") * feature_share
    local_gain = lax.dynamic_slice_in_dim(norm_gain, offset, feature_share, 0).astype(jnp.float32)
    scaled = (widened * local_gain).astype(jnp.bfloat16)
    scaled = lax.all_gather(scaled, "tp", axis=2, tiled=True)
    gathered_squares = lax.all_gather(squares, "section", axis=0, tiled=True)
    scale = lax.rsqrt(gathered_squares / model_width + epsilon)[..., None]
    exchanged = lax.all_to_all(scaled, "grp", split_axis=2, concat_axis=1, tiled=True)
    exchanged = lax.all_gather(exchanged, "section", axis=0, tiled=True)
    seqs, length, depth = exchanged.shape
    flat = exchanged.reshape(seqs * length, depth)

    def project(weight, bias):
        total = jnp.dot(flat, weight, preferred_element_type=jnp.float32).astype(jnp.bfloat16)
        total = total.reshape(seqs, length, -1)
        own = lax.psum_scatter(total, "grp", scatter_dimension=1, tiled=True)
        return (own.astype(jnp.float32) * scale + bias.astype(jnp.float32)).astype(jnp.bfloat16)

    keyval = project(w_keyval, bias_keyval)
    query = project(w_query, bias_query)
    return (hidden, query, keyval)


def solution(mesh):
    placed = (
        P("tp", "section", "grp", None),
        P("section", "grp", "tp"),
        P(),
        P("grp", ("section", "tp")),
        P("grp", ("section", "tp")),
        P(("section", "tp")),
        P(("section", "tp")),
    )
    return jax.shard_map(
        local,
        mesh=mesh,
        in_specs=placed,
        out_specs=(
            P("section", "grp", "tp"),
            P(None, "grp", ("section", "tp")),
            P(None, "grp", ("section", "tp")),
        ),
        check_vma=False,
    )
```

profile of v0, /device:TPU:0, one launch (start us, length us, event | category | flops | bytes accessed | tf_op | source)
XLA Modules:
  0.0 471.7 jit_solution(13430152191114884679)
XLA Ops:
  7.2 0.0 copy-start
  7.2 0.0 copy-start.5
  7.2 0.0 copy-start.3
  7.2 0.0 reduce-scatter.4.cloned.1.call-start
  7.2 0.7 reduce-scatter.4.cloned.1.call-update
  7.9 0.0 all-gather.2.cloned.1.call-start
  8.0 0.0 copy-done.5
  8.0 36.9 %reduce-scatter.4.cloned.1.call-done = bf16[1,128,4096]{2,1,0:T(8,128)(2,1)} async-done(((bf16[1,128,8192]{2,1,0:T(8,128)(2,1)}), bf16[1,128,4096]{2,1,0:T(8,128)(2,1)}) %reduce-scatter.4.cloned.1.call-update) | async-done | bytes 1048592 | tf_op jit(solution)/shard_map/reduce_scatter | solution.py:11
  44.9 0.0 copy-done.3
  44.9 1.7 fusion.1
  46.6 0.0 copy-start.1
  46.6 1.0 copy-done.1
  47.6 1.2 fusion
  48.7 0.0 all-gather.2.cloned.1.call-update
  48.8 0.0 reduce-scatter.8.cloned.1.call-start
  48.8 33.2 %all-gather.2.cloned.1.call-done = bf16[1,128,8192]{2,1,0:T(8,128)(2,1)} async-done(((bf16[1,128,4096]{2,1,0:T(8,128)(2,1)}), bf16[1,128,8192]{2,1,0:T(8,128)(2,1)}) %all-gather.2.cloned.1.call-update) | async-done | bytes 2097168 | tf_op jit(solution)/shard_map/all_gather | solution.py:21
  82.0 9.5 %copy.18 = bf16[1,128,8192]{1,0,2:T(2,128)(2,1)} copy(bf16[1,128,8192]{2,1,0:T(8,128)(2,1)} %all-gather.2.cloned.1.call-done) | data formatting | bytes 4194304 | tf_op jit(solution)/shard_map/all_gather | solution.py:21
  91.5 0.5 broadcast.9
  92.0 45.2 %reduce.1 = bf16[8192,128]{1,0:T(8,128)(2,1)S(1)} reduce(bf16[8192,1,128]{2,1,0:T(2,128)(2,1)} %bitcast.18, bf16[]{:T(256)} %broadcast.9), dimensions={1}, to_apply=%bitcast.12.reduce_sub_computation | reduce | bytes 4194306
  137.2 2.1 reshape.33
  139.3 52.8 %all_to_all.15 = bf16[16,2,32768]{2,1,0:T(2,128)(2,1)S(1)} all-to-all(bf16[16,2,32768]{2,1,0:T(2,128)(2,1)} %reshape.33), channel_id=1, replica_groups=mesh['section'=1,'grp'=16,'tp'=2] {'grp'}, dimensions={0} | all-to-all | bytes 4194304 | tf_op jit(solution)/shard_map/all_to_all | solution.py:24
  192.0 6.8 %reshape.34 = bf16[8192,1,128]{2,1,0:T(2,128)(2,1)} reshape(bf16[16,2,32768]{2,1,0:T(2,128)(2,1)S(1)} %all_to_all.15) | data formatting | bytes 4194304
  198.8 2.5 copy.20
  201.3 2.6 copy.19
  203.9 0.0 copy-done
  203.9 5.9 %convert_bitcast_fusion.1 = bf16[1,2048,1024]{2,1,0:T(8,128)(2,1)} fusion(bf16[2048,512]{1,0:T(8,128)(2,1)} %bitcast.22, bf16[512,1024]{1,0:T(8,128)(2,1)S(1)} %copy-done), kind=kOutput, calls=%fused_computation.1 | convolution fusion | flops 2149580800 | bytes 7340032 | tf_op jit(solution)/shard_map/dot_general | solution.py:30
  209.8 0.0 copy-start.2
  209.8 0.0 reduce-scatter.8.cloned.1.call-update
  209.8 0.2 reduce-scatter.6.cloned.1.call-start
  210.0 1.3 copy-done.2
  211.3 13.8 %convert_bitcast_fusion = bf16[1,2048,4096]{2,1,0:T(8,128)(2,1)} fusion(bf16[2048,512]{1,0:T(8,128)(2,1)S(1)} %bitcast.23, bf16[512,4096]{1,0:T(8,128)(2,1)} %param.10), kind=kOutput, calls=%fused_computation | convolution fusion | flops 8598323200 | bytes 23068672 | tf_op jit(solution)/shard_map/dot_general | solution.py:30
  225.2 0.0 copy-start.6
  225.2 0.0 copy-start.4
  225.2 0.0 reduce-scatter.6.cloned.1.call-update
  225.2 0.7 copy-done.6
  225.9 0.0 copy-done.4
  225.9 4.9 %psum.7 = f32[1,128]{1,0:T(1,128)S(1)} all-reduce(f32[1,128]{1,0:T(1,128)S(1)} %bitcast.24), channel_id=1, replica_groups=mesh['section'=1,'grp'=16,'tp'=2] {'tp'}, use_global_device_ids=true, to_apply=%region_3.0 | all-reduce | flops 128 | bytes 1024 | tf_op jit(solution)/shard_map/psum | solution.py:16
  230.9 51.4 %reduce-scatter.8.cloned.1.call-done = bf16[1,128,1024]{2,1,0:T(8,128)(2,1)} async-done(((bf16[1,2048,1024]{2,1,0:T(8,128)(2,1)}), bf16[1,128,1024]{2,1,0:T(8,128)(2,1)}) %reduce-scatter.8.cloned.1.call-update) | async-done | bytes 262160 | tf_op jit(solution)/shard_map/reduce_scatter | solution.py:32
  282.3 1.8 add_convert_fusion.2
  284.1 178.6 %reduce-scatter.6.cloned.1.call-done = bf16[1,128,4096]{2,1,0:T(8,128)(2,1)} async-done(((bf16[1,2048,4096]{2,1,0:T(8,128)(2,1)}), bf16[1,128,4096]{2,1,0:T(8,128)(2,1)}) %reduce-scatter.6.cloned.1.call-update) | async-done | bytes 1048592 | tf_op jit(solution)/shard_map/reduce_scatter | solution.py:32
  462.6 2.5 add_convert_fusion
  (4 shorter events, 0.0 us)
Async XLA Ops:
  7.2 196.7 %copy-start = (bf16[512,1024]{1,0:T(8,128)(2,1)S(1)}, bf16[512,1024]{1,0:T(8,128)(2,1)}, u32[]{:S(2)}) copy-start(bf16[512,1024]{1,0:T(8,128)(2,1)} %param.11) | copy-start | bytes 3145732
  7.2 0.8 copy-start.5
  7.2 37.7 %copy-start.3 = (bf16[1,128,4096]{2,1,0:T(8,128)(2,1)S(1)}, bf16[1,128,4096]{2,1,0:T(8,128)(2,1)}, u32[]{:S(2)}) copy-start(bf16[1,128,4096]{2,1,0:T(8,128)(2,1)} %param.8) | copy-start | bytes 3145732
  7.2 37.7 %reduce-scatter.4.cloned.1.call-start = ((), (), s32[]{:S(2)}) async-start(), calls=%async_computation.4 | async-start | bytes 3145728 | tf_op jit(solution)/shard_map/reduce_scatter | solution.py:11
  7.9 74.1 %all-gather.2.cloned.1.call-start = ((), (), s32[]{:S(2)}) async-start(), calls=%async_computation.5 | async-start | bytes 3145728 | tf_op jit(solution)/shard_map/all_gather | solution.py:21
  46.6 1.0 copy-start.1
  48.8 233.5 %reduce-scatter.8.cloned.1.call-start = ((), (), s32[]{:S(2)}) async-start(), calls=%async_computation.7 | async-start | bytes 4456448 | tf_op jit(solution)/shard_map/reduce_scatter | solution.py:32
  209.8 1.6 copy-start.2
  209.8 252.9 %reduce-scatter.6.cloned.1.call-start = ((), (), s32[]{:S(2)}) async-start(), calls=%async_computation.6 | async-start | bytes 17825792 | tf_op jit(solution)/shard_map/reduce_scatter | solution.py:32
  225.2 0.7 copy-start.6
  225.2 0.7 copy-start.4
Sparse Core Ops, SparseCore 0:
  10.2 34.6 reduce-scatter.3
  48.9 33.0 all-gather.1
  209.9 72.3 reduce-scatter.7
  286.3 176.3 reduce-scatter.5
where the time goes:
time: 472 us
  waiting for transfers between devices  301 us (64%)
  blocking collectives  57.7 us (12%)
  other arithmetic  52.3 us (11%)
  local copies, waits for them, and re-layouts  26.9 us (6%)
  matrix products  19.7 us (4%)
  between operations  13.8 us (3%)
    reduce_scatter x2, waiting for transfers between devices, project(): own = lax.psum_scatter(total, 'grp', scatter_dimension=1, tiled=True)  230 us
    all_to_all x1, blocking collectives, local(): lax.all_to_all(scaled, 'grp', split_axis=2, concat_axis=1, tiled=True)  52.8 us
    unnamed x1, other arithmetic  45.2 us
    reduce_scatter x1, waiting for transfers between devices, local(): lax.psum_scatter(partials[0], 'tp', scatter_dimension=2, tiled=True)  36.9 us
    all_gather x1, waiting for transfers between devices, local(): scaled = lax.all_gather(scaled, 'tp', axis=2, tiled=True)  33.2 us
    dot_general x2, matrix products, project(): jnp.dot(flat, weight, preferred_element_type=jnp.float32)  19.7 us
    unnamed x18, local copies, waits for them, and re-layouts  14.8 us
    all_gather x1, local copies, waits for them, and re-layouts, local(): scaled = lax.all_gather(scaled, 'tp', axis=2, tiled=True)  9.49 us
  transfers between devices with their start and end apart: 4, of which 4 were waited for; matrix products, arithmetic and copies ran while one was open for 3% of the time, Pallas kernels for 0%

commit v1 on v0

--- a/solution.py
+++ b/solution.py
@@ -21,7 +21,10 @@
     scaled = lax.all_gather(scaled, "tp", axis=2, tiled=True)
     gathered_squares = lax.all_gather(squares, "section", axis=0, tiled=True)
     scale = lax.rsqrt(gathered_squares / model_width + epsilon)[..., None]
-    exchanged = lax.all_to_all(scaled, "grp", split_axis=2, concat_axis=1, tiled=True)
+    exchanged = jnp.concatenate(
+        lax.all_to_all(jnp.stack(jnp.split(scaled, lax.axis_size("grp"), axis=2)), "grp", 0, 0),
+        axis=1,
+    )
     exchanged = lax.all_gather(exchanged, "section", axis=0, tiled=True)
     seqs, length, depth = exchanged.shape
     flat = exchanged.reshape(seqs * length, depth)

time: 472 us -> 415 us (0.88)
  other arithmetic: 52.3 us -> 7.32 us
  local copies, waits for them, and re-layouts: 26.9 us -> 15.4 us
    unnamed x1 -> x0, other arithmetic: 45.2 us -> none
    all_gather x1 -> x0, local copies, waits for them, and re-layouts: 9.49 us -> none  [local(): scaled = lax.all_gather(scaled, 'tp', axis=2, tiled=True)]
    unnamed x18 -> x27, local copies, waits for them, and re-layouts: 14.8 us -> 14.4 us
  transfers between devices with their start and end apart: 4 -> 4, of which waited for: 4 -> 4; matrix products, arithmetic and copies ran while one was open for 3% -> 4% of each run, Pallas kernels for 0% -> 0%
where the time goes in v1:
time: 415 us
  waiting for transfers between devices  302 us (73%)
  blocking collectives  57.5 us (14%)
  matrix products  18.1 us (4%)
  local copies, waits for them, and re-layouts  15.4 us (4%)
  between operations  13.9 us (3%)
  other arithmetic  7.32 us (2%)
    reduce_scatter x2, waiting for transfers between devices, project(): own = lax.psum_scatter(total, 'grp', scatter_dimension=1, tiled=True)  232 us
    all_to_all x1, blocking collectives, local(): lax.all_to_all(jnp.stack(jnp.split(scaled, lax.axis_size('grp'), axis=2))...  52.6 us
    reduce_scatter x1, waiting for transfers between devices, local(): lax.psum_scatter(partials[0], 'tp', scatter_dimension=2, tiled=True)  36.9 us
    all_gather x1, waiting for transfers between devices, local(): scaled = lax.all_gather(scaled, 'tp', axis=2, tiled=True)  33.2 us
    dot_general x2, matrix products, project(): jnp.dot(flat, weight, preferred_element_type=jnp.float32)  18.1 us
    unnamed x27, local copies, waits for them, and re-layouts  14.4 us
  transfers between devices with their start and end apart: 4, of which 4 were waited for; matrix products, arithmetic and copies ran while one was open for 4% of the time, Pallas kernels for 0%

profile of v1, /device:TPU:0, one launch (start us, length us, event | category | flops | bytes accessed | tf_op | source)
XLA Modules:
  0.0 414.7 jit_solution(8445795867458336674)
XLA Ops:
  7.2 0.0 copy-start
  7.2 0.0 copy-start.4
  7.2 0.0 copy-start.2
  7.2 0.0 reduce-scatter.4.cloned.1.call-start
  7.2 0.7 reduce-scatter.4.cloned.1.call-update
  7.9 0.0 all-gather.2.cloned.1.call-start
  8.0 0.0 copy-done.4
  8.0 36.9 %reduce-scatter.4.cloned.1.call-done = bf16[1,128,4096]{2,1,0:T(8,128)(2,1)} async-done(((bf16[1,128,8192]{2,1,0:T(8,128)(2,1)}), bf16[1,128,4096]{2,1,0:T(8,128)(2,1)}) %reduce-scatter.4.cloned.1.call-update) | async-done | bytes 1048592 | tf_op jit(solution)/shard_map/reduce_scatter | solution.py:11
  44.9 0.0 copy-done.2
  44.9 1.7 fusion.1
  46.6 0.0 copy-start.1
  46.6 1.3 fusion
  47.9 0.0 all-gather.2.cloned.1.call-update
  47.9 0.0 reduce-scatter.8.cloned.1.call-start
  48.0 33.2 %all-gather.2.cloned.1.call-done = bf16[1,128,8192]{2,1,0:T(8,128)(2,1)} async-done(((bf16[1,128,4096]{2,1,0:T(8,128)(2,1)}), bf16[1,128,8192]{2,1,0:T(8,128)(2,1)}) %all-gather.2.cloned.1.call-update) | async-done | bytes 2097168 | tf_op jit(solution)/shard_map/all_gather | solution.py:21
  81.2 0.9 fusion.17
  82.1 0.9 fusion.16
  83.0 0.9 fusion.15
  83.9 0.9 fusion.14
  84.9 0.0 copy-done.1
  84.9 0.9 fusion.13
  85.8 0.9 fusion.12
  86.7 0.9 fusion.11
  87.6 0.9 fusion.10
  88.6 0.9 fusion.9
  89.5 0.9 fusion.8
  90.4 0.9 fusion.7
  91.3 0.9 fusion.6
  92.2 0.9 fusion.5
  93.1 0.9 fusion.4
  94.1 0.9 fusion.3
  95.0 0.9 fusion.2
  95.9 52.6 %all_to_all.5 = bf16[16,1,128,512]{3,2,1,0:T(8,128)(2,1)S(1)} all-to-all(bf16[16,1,128,512]{3,2,1,0:T(8,128)(2,1)S(1)} %fusion.2), channel_id=1, replica_groups=mesh['section'=1,'grp'=16,'tp'=2] {'grp'}, dimensions={0} | all-to-all | bytes 4194304 | tf_op jit(solution)/shard_map/all_to_all | solution.py:25
  148.5 0.0 copy-done
  148.5 4.3 %convert_bitcast_fusion.1 = bf16[1,2048,1024]{2,1,0:T(8,128)(2,1)} fusion(bf16[2048,512]{1,0:T(8,128)(2,1)S(1)} %bitcast.78, bf16[512,1024]{1,0:T(8,128)(2,1)S(1)} %copy-done), kind=kOutput, calls=%fused_computation.1 | convolution fusion | flops 2149580800 | bytes 7340032 | tf_op jit(solution)/shard_map/dot_general | solution.py:33
  152.7 0.0 reduce-scatter.8.cloned.1.call-update
  152.8 0.0 reduce-scatter.6.cloned.1.call-start
  152.8 13.9 %convert_bitcast_fusion = bf16[1,2048,4096]{2,1,0:T(8,128)(2,1)} fusion(bf16[2048,512]{1,0:T(8,128)(2,1)S(1)} %bitcast.79, bf16[512,4096]{1,0:T(8,128)(2,1)} %param.10), kind=kOutput, calls=%fused_computation | convolution fusion | flops 8598323200 | bytes 23068672 | tf_op jit(solution)/shard_map/dot_general | solution.py:33
  166.7 0.0 copy-start.5
  166.7 0.0 copy-start.3
  166.7 0.0 reduce-scatter.6.cloned.1.call-update
  166.7 0.7 copy-done.5
  167.4 0.0 copy-done.3
  167.4 4.9 %psum.7 = f32[1,128]{1,0:T(1,128)S(1)} all-reduce(f32[1,128]{1,0:T(1,128)S(1)} %bitcast.80), channel_id=1, replica_groups=mesh['section'=1,'grp'=16,'tp'=2] {'tp'}, use_global_device_ids=true, to_apply=%region_3.0 | all-reduce | flops 128 | bytes 1024 | tf_op jit(solution)/shard_map/psum | solution.py:16
  172.4 52.9 %reduce-scatter.8.cloned.1.call-done = bf16[1,128,1024]{2,1,0:T(8,128)(2,1)} async-done(((bf16[1,2048,1024]{2,1,0:T(8,128)(2,1)}), bf16[1,128,1024]{2,1,0:T(8,128)(2,1)}) %reduce-scatter.8.cloned.1.call-update) | async-done | bytes 262160 | tf_op jit(solution)/shard_map/reduce_scatter | solution.py:35
  225.3 1.8 add_convert_fusion.2
  227.1 178.6 %reduce-scatter.6.cloned.1.call-done = bf16[1,128,4096]{2,1,0:T(8,128)(2,1)} async-done(((bf16[1,2048,4096]{2,1,0:T(8,128)(2,1)}), bf16[1,128,4096]{2,1,0:T(8,128)(2,1)}) %reduce-scatter.6.cloned.1.call-update) | async-done | bytes 1048592 | tf_op jit(solution)/shard_map/reduce_scatter | solution.py:35
  405.7 2.5 add_convert_fusion
  (4 shorter events, 0.0 us)
Async XLA Ops:
  7.2 141.3 %copy-start = (bf16[512,1024]{1,0:T(8,128)(2,1)S(1)}, bf16[512,1024]{1,0:T(8,128)(2,1)}, u32[]{:S(2)}) copy-start(bf16[512,1024]{1,0:T(8,128)(2,1)} %param.11) | copy-start | bytes 3145732
  7.2 0.8 copy-start.4
  7.2 37.7 %copy-start.2 = (bf16[1,128,4096]{2,1,0:T(8,128)(2,1)S(1)}, bf16[1,128,4096]{2,1,0:T(8,128)(2,1)}, u32[]{:S(2)}) copy-start(bf16[1,128,4096]{2,1,0:T(8,128)(2,1)} %param.8) | copy-start | bytes 3145732
  7.2 37.7 %reduce-scatter.4.cloned.1.call-start = ((), (), s32[]{:S(2)}) async-start(), calls=%async_computation.4 | async-start | bytes 3145728 | tf_op jit(solution)/shard_map/reduce_scatter | solution.py:11
  7.9 73.3 %all-gather.2.cloned.1.call-start = ((), (), s32[]{:S(2)}) async-start(), calls=%async_computation.5 | async-start | bytes 3145728 | tf_op jit(solution)/shard_map/all_gather | solution.py:21
  46.6 38.3 %copy-start.1 = (bf16[1,128,4096]{2,1,0:T(8,128)(2,1)}, bf16[1,128,4096]{2,1,0:T(8,128)(2,1)S(1)}, u32[]{:S(2)}) copy-start(bf16[1,128,4096]{2,1,0:T(8,128)(2,1)S(1)} %get-tuple-element.4) | copy-start | bytes 3145732
  47.9 177.3 %reduce-scatter.8.cloned.1.call-start = ((), (), s32[]{:S(2)}) async-start(), calls=%async_computation.7 | async-start | bytes 4456448 | tf_op jit(solution)/shard_map/reduce_scatter | solution.py:35
  152.8 252.9 %reduce-scatter.6.cloned.1.call-start = ((), (), s32[]{:S(2)}) async-start(), calls=%async_computation.6 | async-start | bytes 17825792 | tf_op jit(solution)/shard_map/reduce_scatter | solution.py:35
  166.7 0.7 copy-start.5
  166.7 0.7 copy-start.3
Sparse Core Ops, SparseCore 0:
  10.2 34.6 reduce-scatter.3
  48.1 33.0 all-gather.1
  152.9 72.3 reduce-scatter.7
  229.2 176.3 reduce-scatter.5
